TPU v7x, 32 devices: a whole 2x2x4 slice. The times are simulated.
32 devices in a mesh: ctx: 16 (over z, y, core), head: 2 (over x).
Axes of the slice: x: 2, y: 2, z: 4, core: 2. Of those that a mesh axis runs over, the one named last changes fastest.
Arguments:
- queries: bfloat16 [8192, 16, 128], P('ctx', 'head'), may hold values from -130 to 130, as said below
- values: bfloat16 [8192, 16, 128], P('ctx', 'head'), may hold values from -6 to 6
- codes: int32 [8192, 16], P('ctx', 'head'), may hold values from 0 to 511
- codebook: bfloat16 [16, 512, 128], P('head'), may hold values from -8 to 8, as said below
- out_weight: bfloat16 [2048, 2048], P('head'), may hold values from -0.1875 to 0.1875
Outputs:
- mixed: bfloat16 [8192, 2048], P('ctx', 'head')
Inputs may be any that keep to these rules, and one draw needn't show every extreme that they name: `queries`: every entry has magnitude at most 130. `codebook`: every entry has magnitude at most 8.
All inputs are finite; a program needn't handle non-finite values.
Results may differ from a plain program's by a relative error of at most 0.0066.
Values may be sent and summed in bfloat16 or wider, within the bound.
No kernel may reach another device: no remote copies, remote signals or barrier semaphores. Data moves between devices by JAX's collectives and lax.ppermute only.
A program may use at most 128 MiB of HBM per device.

v0:
```python
import jax
import jax.numpy as jnp
from jax import lax
from jax.sharding import PartitionSpec as P

BLOCK = 512


def from_behind(value, axis, steps):
    count = lax.axis_size(axis)
    first, last = (max(0, -steps), min(count, count - steps))
    return lax.ppermute(value, axis, [(source, source + steps) for source in range(first, last)])


def prefix(x, axis, combine, identity):
    devices, here = (lax.axis_size(axis), lax.axis_index(axis))
    everything = jax.tree.map(lambda part: lax.all_gather(part, axis), x)
    start = jax.tree.map(
        lambda part, zero: jnp.broadcast_to(jnp.asarray(zero, part.dtype), part.shape), x, identity
    )

    def turn(k, before):
        reached = k < here
        new = combine(before, jax.tree.map(lambda part: part[k], everything))
        return jax.tree.map(lambda a, b: jnp.where(reached, a, b), new, before)

    return lax.fori_loop(0, devices, turn, start)


def attend(query, cur_keys, cur_values, prev_keys, prev_values, live, book, cache_sum, cache_count):
    scale = query.shape[-1] ** (-0.5)
    code_scores = jnp.dot(query, book.T, preferred_element_type=jnp.float32) * scale
    cur_scores = jnp.dot(query, cur_keys.T, preferred_element_type=jnp.float32) * scale
    prev_scores = jnp.dot(query, prev_keys.T, preferred_element_type=jnp.float32) * scale
    rows = lax.broadcasted_iota(jnp.int32, cur_scores.shape, 0)
    cols = lax.broadcasted_iota(jnp.int32, cur_scores.shape, 1)
    causal = rows >= cols
    present = (cache_count > 0.0)[None, :]
    top = jnp.max(jnp.where(causal, cur_scores, -jnp.inf), axis=1)
    top = jnp.maximum(top, jnp.max(jnp.where(live, prev_scores, -jnp.inf), axis=1))
    top = jnp.maximum(top, jnp.max(jnp.where(present, code_scores, -jnp.inf), axis=1))
    top = top[:, None]
    cur_weight = jnp.where(causal, jnp.exp(cur_scores - top), 0.0)
    prev_weight = jnp.where(live, jnp.exp(prev_scores - top), 0.0)
    code_weight = jnp.where(present, jnp.exp(code_scores - top), 0.0)
    denom = (
        jnp.sum(cur_weight, axis=1)
        + jnp.sum(prev_weight, axis=1)
        + jnp.sum(code_weight * cache_count[None, :], axis=1)
    )
    numer = jnp.dot(cur_weight.astype(jnp.bfloat16), cur_values, preferred_element_type=jnp.float32)
    numer = numer + jnp.dot(
        prev_weight.astype(jnp.bfloat16), prev_values, preferred_element_type=jnp.float32
    )
    numer = numer + jnp.dot(code_weight, cache_sum, precision=lax.Precision.HIGHEST)
    return (numer / denom[:, None]).astype(jnp.bfloat16)


def add_totals(earlier, later):
    return (earlier[0] + later[0], earlier[1] + later[1])


def on_device(queries, values, codes, codebook, out_weight):
    tokens, local_heads, width = queries.shape
    ncodes = codebook.shape[1]
    nblocks = tokens // BLOCK
    keys = jax.vmap(lambda book, index: book[index], in_axes=(0, 1), out_axes=1)(codebook, codes)
    table = lax.broadcasted_iota(jnp.int32, (1, 1, ncodes), 2)
    onehot = (
        (codes[:, :, None] == table)
        .astype(jnp.bfloat16)
        .reshape(nblocks, BLOCK, local_heads, ncodes)
    )
    block_sums = jnp.einsum(
        "bths,bthd->bhsd",
        onehot,
        values.reshape(nblocks, BLOCK, local_heads, width),
        preferred_element_type=jnp.float32,
    )
    block_counts = jnp.sum(onehot.astype(jnp.float32), axis=1)
    last_sum, last_count = (block_sums[nblocks - 1], block_counts[nblocks - 1])
    rest_sum = jnp.sum(block_sums[: nblocks - 1], axis=0)
    rest_count = jnp.sum(block_counts[: nblocks - 1], axis=0)
    prev_keys, prev_values = from_behind((keys, values), "ctx", 1)
    zero_sum = jnp.zeros_like(last_sum)
    zero_count = jnp.zeros_like(last_count)
    total_sum, total_count = prefix(
        (rest_sum + last_sum, rest_count + last_count), "ctx", add_totals, (zero_sum, zero_count)
    )
    pend_sum, pend_count = from_behind((last_sum, last_count), "ctx", 1)
    cache_sum = total_sum - pend_sum
    cache_count = total_count - pend_count
    live = lax.axis_index("ctx") > 0
    attended = jax.vmap(attend, in_axes=(1, 1, 1, 1, 1, None, 0, 0, 0), out_axes=1)(
        queries, keys, values, prev_keys, prev_values, live, codebook, cache_sum, cache_count
    )
    attended_all = attended.reshape(tokens, local_heads * width)
    columns = lax.all_to_all(out_weight, "head", split_axis=1, concat_axis=0, tiled=True)
    summed = jnp.dot(
        lax.all_gather(attended_all, "head", axis=1, tiled=True),
        columns,
        preferred_element_type=jnp.float32,
    )
    return summed.astype(jnp.bfloat16)


def solution(mesh):
    return jax.shard_map(
        on_device,
        mesh=mesh,
        in_specs=(
            P("ctx", "head", None),
            P("ctx", "head", None),
            P("ctx", "head"),
            P("head", None, None),
            P("head", None),
        ),
        out_specs=P("ctx", "head"),
        check_vma=False,
    )
```

profile of v0, /device:TPU:0, one launch (start us, length us, event | category | flops | bytes accessed | tf_op | source)
XLA Modules:
  0.0 355.7 jit_solution(16759261698368009623)
XLA Ops:
  6.5 2.5 copy.66
  9.0 4.0 %fusion.3 = f32[8,512,128]{2,1,0:T(8,128)} fusion(bf16[512,8,128]{0,2,1:T(8,128)(2,1)} %copy.66, s32[512,8]{0,1:T(8,128)} %param.9), kind=kOutput, calls=%fused_computation.18 | convolution fusion | flops 538968064 | bytes 3162112 | tf_op jit(solution)/shard_map/bths,bthd->bhsd/dot_general | solution.py:74
  13.1 40.2 %gather_fusion = bf16[4096,128]{1,0:T(8,128)(2,1)} fusion(bf16[8,512,128]{2,1,0:T(8,128)(2,1)S(1)} %copy-done, s32[4096]{0:T(1024)S(1)} %bitcast.65), kind=kCustom, calls=%fused_computation | custom fusion | bytes 2129920 | tf_op jit(solution)/shard_map/vmap()/gather | solution.py:67
  53.3 3.4 collective-permute-start
  56.6 4.5 %collective-permute-start.2 = (bf16[512,8,128]{0,2,1:T(8,128)(2,1)}, bf16[512,8,128]{0,2,1:T(8,128)(2,1)}, u32[]{:S(2)}, u32[]{:S(2)}) collective-permute-start(bf16[512,8,128]{0,2,1:T(8,128)(2,1)} %copy.66), channel_id=1, source_target_pairs={{0,2},{2,4},{4,6},{6,8},{8,10},{10,12},{12,14},{14,16},{16,18},{18... | collective-permute-start | bytes 3145736 | tf_op jit(solution)/shard_map/ppermute | solution.py:12
  61.2 2.6 collective-permute-start.3
  63.9 1.0 convert_reduce_fusion
  64.9 1.9 collective-permute-start.1
  66.8 6.5 %copy.70 = bf16[1024,2048]{0,1:T(8,128)(2,1)} copy(bf16[1024,2048]{1,0:T(8,128)(2,1)} %param.11) | data formatting | bytes 8388608 | tf_op args[4]
  73.2 5.6 %all-to-all-start = ((bf16[1024,2,1024]{0,2,1:T(8,128)(2,1)}), bf16[1024,2,1024]{0,2,1:T(8,128)(2,1)}, u32[]{:S(2)}, u32[]{:S(2)}) async-start(bf16[1024,2,1024]{0,2,1:T(8,128)(2,1)} %bitcast.70), calls=%async_computation | async-start | bytes 8388608 | tf_op jit(solution)/shard_map/all_to_all | solution.py:98
  79.0 132.5 %all-gather.1 = f32[128,512]{1,0:T(8,128)} all-gather(f32[8,512]{1,0:T(8,128)S(1)} %convert_reduce_fusion), channel_id=3, replica_groups=mesh['ctx'=16,'head'=2] {'ctx'}, dimensions={0}, use_global_device_ids=true | all-gather | bytes 278528 | tf_op jit(solution)/shard_map/all_gather | solution.py:17
  211.5 6.2 %fusion = (f32[8,512]{1,0:T(8,128)S(1)}, f32[8,512,512]{2,1,0:T(8,128)}) fusion(pred[512,512]{0,1:T(8,128)(4,1)S(1)} %iota_compare_fusion.3, bf16[8,512,128]{2,1,0:T(8,128)(2,1)} %bitcast.2, bf16[512,8,128]{2,1,0:T(8,128)(2,1)} %param.7), kind=kOutput, calls=%fused_computation.7 | convolution fusion | flops 543158272 | bytes 10764288 | tf_op jit(solution)/shard_map/vmap()/dot_general | solution.py:33
  217.7 5.7 %select_reduce_fusion.1 = (f32[8,512]{1,0:T(8,128)S(1)}, f32[8,512,512]{1,2,0:T(8,128)}) fusion(pred[]{:T(512)S(6)} %gt.6, bf16[512,8,128]{2,1,0:T(8,128)(2,1)S(1)} %copy-done.2, bf16[512,8,128]{2,0,1:T(8,128)(2,1)} %collective-permute-done), kind=kOutput, calls=%fused_computation.17 | convolution fusion | flops 543158272 | bytes 10502145 | tf_op jit(solution)/shard_map/vmap()/dot_general | solution.py:34
  223.4 3.9 %all-gather.7.cloned.1.call-done = f32[128,512,128]{2,1,0:T(8,128)} async-done(((f32[8,512,128]{2,1,0:T(8,128)}), f32[128,512,128]{2,1,0:T(8,128)}) %all-gather.7.cloned.1.call-update) | async-done | bytes 33554448 | tf_op jit(solution)/shard_map/all_gather | solution.py:17
  227.3 48.6 %while.16 = (s32[]{:T(128)}, f32[8,512,128]{2,1,0:T(8,128)S(1)}, f32[8,512]{1,0:T(8,128)S(1)}, s32[]{:T(128)}, f32[16,8,512,128]{3,2,1,0:T(8,128)}, /*index=5*/f32[16,8,512]{2,1,0:T(8,128)}, s32[]{:T(128)}, s32[]{:T(128)}) while((s32[]{:T(128)}, f32[8,512,128]{2,1,0:T(8,128)S(1)}, f32[8,512]{1,0:T(8,128)S(1)}, s32[]{:T(128)}, ...), condition=%wide.region_4.5_spmd.clone, body=%wide.region_3.4_spmd.clone.sunk | while | flops 1585156 | bytes 6340723 | solution.py:27
  227.3 2.3 add_select_fusion.4
  229.6 0.7 add_select_fusion.5
  230.4 2.3 add_select_fusion.4
  232.7 0.7 add_select_fusion.5
  233.4 2.3 add_select_fusion.4
  235.7 0.7 add_select_fusion.5
  236.4 2.3 add_select_fusion.4
  238.8 0.7 add_select_fusion.5
  239.5 2.3 add_select_fusion.4
  241.8 0.7 add_select_fusion.5
  242.5 2.3 add_select_fusion.4
  244.8 0.7 add_select_fusion.5
  245.5 2.3 add_select_fusion.4
  247.9 0.7 add_select_fusion.5
  248.6 2.3 add_select_fusion.4
  251.6 2.3 add_select_fusion.4
  254.7 2.3 add_select_fusion.4
  257.7 2.3 add_select_fusion.4
  260.7 2.3 add_select_fusion.4
  263.8 2.3 add_select_fusion.4
  266.8 2.3 add_select_fusion.4
  269.8 2.3 add_select_fusion.4
  272.9 2.3 add_select_fusion.4
  275.2 0.7 add_select_fusion.5
  275.9 3.5 select_reduce_fusion
  279.5 7.9 %fusion.6 = (f32[8,512]{1,0:T(8,128)S(1)}, f32[8,512]{1,0:T(8,128)S(1)}) fusion(f32[8,512,512]{2,1,0:T(8,128)} %get-tuple-element.157, f32[8,512]{1,0:T(8,128)S(1)} %maximum_maximum_fusion, pred[512,512]{0,1:T(8,128)(4,1)S(1)} %iota_compare_fusion.3, f32[8,512]{1,0:T(8,128)S(1)} %get-tuple-element.153, f32[8,512,512]{1,2,0:T(8,128)S(1)} %get-tuple-element.155, ...), kind=kLoop, calls=%fused_computation.21 | loop fusion | flops 18866176 | bytes 17108992 | tf_op jit(solution)/shard_map/vmap()/reduce_sum | solution.py:47
  287.4 2.2 bitcast_reduce_fusion
  289.6 3.3 fusion.8
  292.9 3.2 fusion.10
  296.1 9.2 %fusion.24 = bf16[512,8,128]{0,2,1:T(8,128)(2,1)} fusion(f32[8,512,128]{1,2,0:T(8,128)S(1)} %fusion.8, f32[8,512,128]{1,2,0:T(8,128)S(1)} %fusion.10, f32[512,8]{0,1:T(8,128)S(1)} %add_bitcast_fusion, f32[8,512,128]{2,1,0:T(8,128)S(1)} %get-tuple-element.116, f32[8,512,128]{2,1,0:T(8,128)} %collective-permute-done.3, ...), kind=kOutput, calls=%fused_computation.39 | convolution fusion | flops 3230138368 | bytes 17862656 | tf_op jit(solution)/shard_map/vmap()/dot_general | solution.py:55
  305.3 6.3 %copy.71 = bf16[2,1024,1024]{2,1,0:T(8,128)(2,1)} copy(bf16[2,1024,1024]{1,2,0:T(8,128)(2,1)} %bitcast.13) | data formatting | bytes 8388608 | tf_op jit(solution)/shard_map/all_to_all | solution.py:98
  311.6 31.1 %all-gather.5.cloned.1.call-done = bf16[512,2048]{0,1:T(8,128)(2,1)} async-done(((bf16[512,1024]{0,1:T(8,128)(2,1)}), bf16[512,2048]{0,1:T(8,128)(2,1)}) %all-gather.5.cloned.1.call-update) | async-done | bytes 2097168 | tf_op jit(solution)/shard_map/all_gather | solution.py:100
  342.8 6.1 %convolution_convert_fusion = bf16[512,1024]{1,0:T(8,128)(2,1)} fusion(bf16[512,2048]{0,1:T(8,128)(2,1)} %all-gather.5.cloned.1.call-done, bf16[2048,1024]{1,0:T(8,128)(2,1)} %bitcast.71), kind=kOutput, calls=%fused_computation.41 | convolution fusion | flops 2148007936 | bytes 7340032 | tf_op jit(solution)/shard_map/dot_general | solution.py:99
  (44 shorter events, 6.2 us)
Async XLA Ops:
  6.5 6.6 %copy-start = (bf16[8,512,128]{2,1,0:T(8,128)(2,1)S(1)}, bf16[8,512,128]{2,1,0:T(8,128)(2,1)}, u32[]{:S(2)}) copy-start(bf16[8,512,128]{2,1,0:T(8,128)(2,1)} %param.10) | copy-start | bytes 3145732
  6.5 6.5 %copy-start.3 = (s32[512,8]{0,1:T(8,128)S(1)}, s32[512,8]{0,1:T(8,128)}, u32[]{:S(2)}) copy-start(s32[512,8]{0,1:T(8,128)} %param.9) | copy-start | bytes 49156
  6.5 220.8 %all-gather.7.cloned.1.call-start = ((), (), s32[]{:S(2)}) async-start(), calls=%async_computation.2 | async-start | bytes 35651584 | tf_op jit(solution)/shard_map/all_gather | solution.py:17
  53.3 164.5 %collective-permute-start = (bf16[512,8,128]{2,0,1:T(8,128)(2,1)}, bf16[512,8,128]{2,0,1:T(8,128)(2,1)}, u32[]{:S(2)}, u32[]{:S(2)}) collective-permute-start(bf16[512,8,128]{2,0,1:T(8,128)(2,1)} %bitcast.4), channel_id=1, source_target_pairs={{0,2},{2,4},{4,6},{6,8},{8,10},{10,12},{12,14},{14,16},{16,18},{18... | collective-permute-start | bytes 3145736 | tf_op jit(solution)/shard_map/ppermute | solution.py:12
  56.6 236.2 %collective-permute-start.2 = (bf16[512,8,128]{0,2,1:T(8,128)(2,1)}, bf16[512,8,128]{0,2,1:T(8,128)(2,1)}, u32[]{:S(2)}, u32[]{:S(2)}) collective-permute-start(bf16[512,8,128]{0,2,1:T(8,128)(2,1)} %copy.66), channel_id=1, source_target_pairs={{0,2},{2,4},{4,6},{6,8},{8,10},{10,12},{12,14},{14,16},{16,18},{18... | collective-permute-start | bytes 3145736 | tf_op jit(solution)/shard_map/ppermute | solution.py:12
  61.2 234.9 %collective-permute-start.3 = (f32[8,512,128]{2,1,0:T(8,128)}, f32[8,512,128]{2,1,0:T(8,128)}, u32[]{:S(2)}, u32[]{:S(2)}) collective-permute-start(f32[8,512,128]{2,1,0:T(8,128)} %fusion.3), channel_id=1, source_target_pairs={{0,2},{2,4},{4,6},{6,8},{8,10},{10,12},{12,14},{14,16},{16,18},{18... | collective-permute-start | bytes 6291464 | tf_op jit(solution)/shard_map/ppermute | solution.py:12
  64.9 211.0 %collective-permute-start.1 = (f32[8,512]{1,0:T(8,128)S(1)}, f32[8,512]{1,0:T(8,128)S(1)}, u32[]{:S(2)}, u32[]{:S(2)}) collective-permute-start(f32[8,512]{1,0:T(8,128)S(1)} %convert_reduce_fusion), channel_id=1, source_target_pairs={{0,2},{2,4},{4,6},{6,8},{8,10},{10,12},{12,14},{14,16},{16,18},{18... | collective-permute-start | bytes 49160 | tf_op jit(solution)/shard_map/ppermute | solution.py:12
  73.2 232.1 %all-to-all-start = ((bf16[1024,2,1024]{0,2,1:T(8,128)(2,1)}), bf16[1024,2,1024]{0,2,1:T(8,128)(2,1)}, u32[]{:S(2)}, u32[]{:S(2)}) async-start(bf16[1024,2,1024]{0,2,1:T(8,128)(2,1)} %bitcast.70), calls=%async_computation | async-start | bytes 8388608 | tf_op jit(solution)/shard_map/all_to_all | solution.py:98
  78.8 263.9 %all-gather.5.cloned.1.call-start = ((), (), s32[]{:S(2)}) async-start(), calls=%async_computation.1 | async-start | bytes 3145728 | tf_op jit(solution)/shard_map/all_gather | solution.py:100
  78.9 138.8 %copy-start.2 = (bf16[512,8,128]{2,1,0:T(8,128)(2,1)S(1)}, bf16[512,8,128]{2,1,0:T(8,128)(2,1)}, u32[]{:S(2)}) copy-start(bf16[512,8,128]{2,1,0:T(8,128)(2,1)} %param.7) | copy-start | bytes 3145732
  275.9 11.5 %slice-start.2 = ((s8[8388608]{0:T(1024)(128)(4,1)}), s8[4194304]{0:T(1024)(128)(4,1)S(1)}, s32[]{:S(2)}) async-start(s8[8388608]{0:T(1024)(128)(4,1)} %bitcast.68), calls=%async_computation.5 | async-start | bytes 8388608
  275.9 13.7 %slice-start = ((s8[8388608]{0:T(1024)(128)(4,1)}), s8[4194304]{0:T(1024)(128)(4,1)S(1)}, s32[]{:S(2)}) async-start(s8[8388608]{0:T(1024)(128)(4,1)} %bitcast.66), calls=%async_computation.3 | async-start | bytes 8388608
  279.4 7.9 %slice-start.3 = ((s8[8388608]{0:T(1024)(128)(4,1)}), s8[4194304]{0:T(1024)(128)(4,1)S(1)}, s32[]{:S(2)}) async-start(s8[8388608]{0:T(1024)(128)(4,1)} %bitcast.68), calls=%async_computation.6 | async-start | bytes 8388608
  279.4 10.1 %slice-start.1 = ((s8[8388608]{0:T(1024)(128)(4,1)}), s8[4194304]{0:T(1024)(128)(4,1)S(1)}, s32[]{:S(2)}) async-start(s8[8388608]{0:T(1024)(128)(4,1)} %bitcast.66), calls=%async_computation.4 | async-start | bytes 8388608
  305.3 43.6 %copy-start.1 = (bf16[8,512,128]{2,1,0:T(8,128)(2,1)S(1)}, bf16[8,512,128]{2,1,0:T(8,128)(2,1)}, u32[]{:S(2)}) copy-start(bf16[8,512,128]{2,1,0:T(8,128)(2,1)} %param.10) | copy-start | bytes 3145732
Sparse Core Ops, SparseCore 0:
  13.2 214.1 all-gather.6
  305.4 37.2 all-gather.4
where the time goes:
time: 358 us; the launch traced here: 356 us
  blocking collectives  132 us (37%)
  other arithmetic  59.6 us (17%)
  local copies, waits for them, and re-layouts  55.6 us (16%)
  matrix products  41.2 us (12%)
  waiting for transfers between devices  35.1 us (10%)
  starting transfers between devices  18 us (5%)
  between operations  13.7 us (4%)
    all_gather x1, blocking collectives, prefix(): everything = jax.tree.map(lambda part: lax.all_gather(part, axis), x)  132 us
    select_n x32, other arithmetic, turn(): return jax.tree.map(lambda a, b: jnp.where(reached, a, b), new, before)  48.5 us
    gather x1, local copies, waits for them, and re-layouts, on_device(): book[index]  40.2 us
    all_gather x1, waiting for transfers between devices, on_device(): lax.all_gather(attended_all, 'head', axis=1, tiled=True)  31.1 us
    ppermute x4, starting transfers between devices, from_behind(): lax.ppermute(value, axis, [(source, source + steps) for source in range(f...  12.4 us
    dot_general x1, matrix products, attend(): jnp.dot(code_weight, cache_sum, precision=lax.Precision.HIGHEST)  9.17 us
    unnamed x20, local copies, waits for them, and re-layouts  9.13 us
    reduce_sum x1, other arithmetic, attend(): jnp.sum(cur_weight, axis=1) + jnp.sum(prev_weight, axis=1)  7.9 us
  transfers between devices with their start and end apart: 7, of which 2 were waited for; matrix products, arithmetic and copies ran while one was open for 40% of the time, Pallas kernels for 0%

commit v1 on v0

--- a/solution.py
+++ b/solution.py
@@ -97,7 +97,7 @@
     attended_all = attended.reshape(tokens, local_heads * width)
     columns = lax.all_to_all(out_weight, "head", split_axis=1, concat_axis=0, tiled=True)
     summed = jnp.dot(
-        lax.all_gather(attended_all, "head", axis=1, tiled=True),
+        jnp.concatenate(lax.all_gather(attended_all, "head"), axis=1),
         columns,
         preferred_element_type=jnp.float32,
     )

time: 358 us -> 358 us (level)
  waiting for transfers between devices: 35.1 us -> 41.4 us
  blocking collectives: 132 us -> 126 us
    all_gather x1, blocking collectives: 132 us -> 126 us  [prefix(): everything = jax.tree.map(lambda part: lax.all_gather(part, axis), x)]
    all_gather x1, waiting for transfers between devices: 31.1 us -> 37.4 us  [on_device(): lax.all_gather(attended_all, 'head')]
where the time goes in v1:
time: 358 us; the launch traced here: 356 us
  blocking collectives  126 us (35%)
  other arithmetic  59.6 us (17%)
  local copies, waits for them, and re-layouts  56.9 us (16%)
  waiting for transfers between devices  41.4 us (12%)
  matrix products  40.4 us (11%)
  starting transfers between devices  18.2 us (5%)
  between operations  13.7 us (4%)
    all_gather x1, blocking collectives, prefix(): everything = jax.tree.map(lambda part: lax.all_gather(part, axis), x)  126 us
    select_n x32, other arithmetic, turn(): return jax.tree.map(lambda a, b: jnp.where(reached, a, b), new, before)  48.5 us
    gather x1, local copies, waits for them, and re-layouts, on_device(): book[index]  40.2 us
    all_gather x1, waiting for transfers between devices, on_device(): lax.all_gather(attended_all, 'head')  37.4 us
    ppermute x4, starting transfers between devices, from_behind(): lax.ppermute(value, axis, [(source, source + steps) for source in range(f...  12.4 us
    unnamed x20, local copies, waits for them, and re-layouts  9.16 us
    dot_general x1, matrix products, attend(): jnp.dot(code_weight, cache_sum, precision=lax.Precision.HIGHEST)  8.39 us
    reduce_sum x1, other arithmetic, attend(): jnp.sum(cur_weight, axis=1) + jnp.sum(prev_weight, axis=1)  7.9 us
  transfers between devices with their start and end apart: 7, of which 2 were waited for; matrix products, arithmetic and copies ran while one was open for 40% of the time, Pallas kernels for 0%

profile of v1, /device:TPU:0, one launch (start us, length us, event | category | flops | bytes accessed | tf_op | source)
XLA Modules:
  0.0 356.3 jit_solution(2032987843232831951)
XLA Ops:
  6.5 2.5 copy.57
  9.0 4.0 %fusion.3 = f32[8,512,128]{2,1,0:T(8,128)} fusion(bf16[512,8,128]{0,2,1:T(8,128)(2,1)} %copy.57, s32[512,8]{0,1:T(8,128)} %param.9), kind=kOutput, calls=%fused_computation.18 | convolution fusion | flops 538968064 | bytes 3162112 | tf_op jit(solution)/shard_map/bths,bthd->bhsd/dot_general | solution.py:74
  13.1 40.2 %gather_fusion = bf16[4096,128]{1,0:T(8,128)(2,1)} fusion(bf16[8,512,128]{2,1,0:T(8,128)(2,1)S(1)} %copy-done, s32[4096]{0:T(1024)S(1)} %bitcast.73), kind=kCustom, calls=%fused_computation | custom fusion | bytes 2129920 | tf_op jit(solution)/shard_map/vmap()/gather | solution.py:67
  53.3 3.4 collective-permute-start
  56.6 4.5 %collective-permute-start.2 = (bf16[512,8,128]{0,2,1:T(8,128)(2,1)}, bf16[512,8,128]{0,2,1:T(8,128)(2,1)}, u32[]{:S(2)}, u32[]{:S(2)}) collective-permute-start(bf16[512,8,128]{0,2,1:T(8,128)(2,1)} %copy.57), channel_id=1, source_target_pairs={{0,2},{2,4},{4,6},{6,8},{8,10},{10,12},{12,14},{14,16},{16,18},{18... | collective-permute-start | bytes 3145736 | tf_op jit(solution)/shard_map/ppermute | solution.py:12
  61.2 2.6 collective-permute-start.3
  63.9 1.0 convert_reduce_fusion
  64.9 1.9 collective-permute-start.1
  66.8 6.5 %copy.62 = bf16[1024,2048]{0,1:T(8,128)(2,1)} copy(bf16[1024,2048]{1,0:T(8,128)(2,1)} %param.11) | data formatting | bytes 8388608 | tf_op args[4]
  73.3 6.2 %copy.63 = bf16[1024,2,1024]{2,0,1:T(8,128)(2,1)} copy(bf16[1024,2,1024]{0,2,1:T(8,128)(2,1)} %bitcast.78) | data formatting | bytes 8388608 | tf_op jit(solution)/shard_map/all_to_all | solution.py:98
  79.5 5.8 %all-to-all-start = ((bf16[1024,2,1024]{2,0,1:T(8,128)(2,1)}), bf16[1024,2,1024]{2,0,1:T(8,128)(2,1)}, u32[]{:S(2)}, u32[]{:S(2)}) async-start(bf16[1024,2,1024]{2,0,1:T(8,128)(2,1)} %copy.63), calls=%async_computation | async-start | bytes 8388608 | tf_op jit(solution)/shard_map/all_to_all | solution.py:98
  85.4 126.1 %all-gather.1 = f32[128,512]{1,0:T(8,128)} all-gather(f32[8,512]{1,0:T(8,128)S(1)} %convert_reduce_fusion), channel_id=3, replica_groups=mesh['ctx'=16,'head'=2] {'ctx'}, dimensions={0}, use_global_device_ids=true | all-gather | bytes 278528 | tf_op jit(solution)/shard_map/all_gather | solution.py:17
  211.5 6.2 %fusion = (f32[8,512]{1,0:T(8,128)S(1)}, f32[8,512,512]{2,1,0:T(8,128)}) fusion(pred[512,512]{0,1:T(8,128)(4,1)S(1)} %iota_compare_fusion.3, bf16[8,512,128]{2,1,0:T(8,128)(2,1)} %bitcast.2, bf16[512,8,128]{2,1,0:T(8,128)(2,1)} %param.7), kind=kOutput, calls=%fused_computation.7 | convolution fusion | flops 543158272 | bytes 10764288 | tf_op jit(solution)/shard_map/vmap()/dot_general | solution.py:33
  217.7 5.7 %select_reduce_fusion.1 = (f32[8,512]{1,0:T(8,128)S(1)}, f32[8,512,512]{1,2,0:T(8,128)}) fusion(pred[]{:T(512)S(6)} %gt.6, bf16[512,8,128]{2,1,0:T(8,128)(2,1)S(1)} %copy-done.2, bf16[512,8,128]{2,0,1:T(8,128)(2,1)} %collective-permute-done), kind=kOutput, calls=%fused_computation.17 | convolution fusion | flops 543158272 | bytes 10502145 | tf_op jit(solution)/shard_map/vmap()/dot_general | solution.py:34
  223.4 3.9 %all-gather.7.cloned.1.call-done = f32[128,512,128]{2,1,0:T(8,128)} async-done(((f32[8,512,128]{2,1,0:T(8,128)}), f32[128,512,128]{2,1,0:T(8,128)}) %all-gather.7.cloned.1.call-update) | async-done | bytes 33554448 | tf_op jit(solution)/shard_map/all_gather | solution.py:17
  227.3 48.6 %while.16 = (s32[]{:T(128)}, f32[8,512,128]{2,1,0:T(8,128)S(1)}, f32[8,512]{1,0:T(8,128)S(1)}, s32[]{:T(128)}, f32[16,8,512,128]{3,2,1,0:T(8,128)}, /*index=5*/f32[16,8,512]{2,1,0:T(8,128)}, s32[]{:T(128)}, s32[]{:T(128)}) while((s32[]{:T(128)}, f32[8,512,128]{2,1,0:T(8,128)S(1)}, f32[8,512]{1,0:T(8,128)S(1)}, s32[]{:T(128)}, ...), condition=%wide.region_4.5_spmd.clone, body=%wide.region_3.4_spmd.clone.sunk | while | flops 1585156 | bytes 6340723 | solution.py:27
  227.3 2.3 add_select_fusion.4
  229.6 0.7 add_select_fusion.5
  230.4 2.3 add_select_fusion.4
  232.7 0.7 add_select_fusion.5
  233.4 2.3 add_select_fusion.4
  235.7 0.7 add_select_fusion.5
  236.4 2.3 add_select_fusion.4
  238.8 0.7 add_select_fusion.5
  239.5 2.3 add_select_fusion.4
  241.8 0.7 add_select_fusion.5
  242.5 2.3 add_select_fusion.4
  244.8 0.7 add_select_fusion.5
  245.5 2.3 add_select_fusion.4
  248.6 2.3 add_select_fusion.4
  251.6 2.3 add_select_fusion.4
  254.7 2.3 add_select_fusion.4
  257.7 2.3 add_select_fusion.4
  260.7 2.3 add_select_fusion.4
  263.8 2.3 add_select_fusion.4
  266.8 2.3 add_select_fusion.4
  269.8 2.3 add_select_fusion.4
  272.9 2.3 add_select_fusion.4
  275.2 0.7 add_select_fusion.5
  275.9 3.5 select_reduce_fusion
  279.5 7.9 %fusion.6 = (f32[8,512]{1,0:T(8,128)S(1)}, f32[8,512]{1,0:T(8,128)S(1)}) fusion(f32[8,512,512]{2,1,0:T(8,128)} %get-tuple-element.157, f32[8,512]{1,0:T(8,128)S(1)} %maximum_maximum_fusion, pred[512,512]{0,1:T(8,128)(4,1)S(1)} %iota_compare_fusion.3, f32[8,512]{1,0:T(8,128)S(1)} %get-tuple-element.153, f32[8,512,512]{1,2,0:T(8,128)S(1)} %get-tuple-element.155, ...), kind=kLoop, calls=%fused_computation.21 | loop fusion | flops 18866176 | bytes 17108992 | tf_op jit(solution)/shard_map/vmap()/reduce_sum | solution.py:47
  287.4 2.2 bitcast_reduce_fusion
  289.6 3.3 fusion.8
  292.9 3.2 fusion.10
  296.1 8.4 %fusion.27 = bf16[512,8,128]{0,2,1:T(8,128)(2,1)S(1)} fusion(f32[8,512,128]{1,2,0:T(8,128)S(1)} %fusion.8, f32[8,512,128]{1,2,0:T(8,128)S(1)} %fusion.10, f32[512,8]{0,1:T(8,128)S(1)} %add_bitcast_fusion, f32[8,512,128]{2,1,0:T(8,128)S(1)} %get-tuple-element.116, f32[8,512,128]{2,1,0:T(8,128)} %collective-permute-done.3, ...), kind=kOutput, calls=%fused_computation.43 | convolution fusion | flops 3230138368 | bytes 17862656 | tf_op jit(solution)/shard_map/vmap()/dot_general | solution.py:55
  304.5 1.3 copy.61
  305.9 37.4 %all-gather.5.cloned.1.call-done = bf16[2,512,1024]{2,1,0:T(8,128)(2,1)} async-done(((bf16[1,512,1024]{2,1,0:T(8,128)(2,1)}), bf16[2,512,1024]{2,1,0:T(8,128)(2,1)}) %all-gather.5.cloned.1.call-update) | async-done | bytes 2097168 | tf_op jit(solution)/shard_map/all_gather | solution.py:100
  343.3 6.1 %bitcast_convert_fusion.2 = bf16[512,1024]{1,0:T(8,128)(2,1)} fusion(bf16[1024,2,1024]{2,0,1:T(8,128)(2,1)} %all-to-all-done, bf16[2,512,1024]{2,1,0:T(8,128)(2,1)} %all-gather.5.cloned.1.call-done), kind=kOutput, calls=%fused_computation.40 | convolution fusion | flops 2148007936 | bytes 7340032 | tf_op jit(solution)/shard_map/dot_general | solution.py:99
  (45 shorter events, 6.9 us)
Async XLA Ops:
  6.5 6.6 %copy-start = (bf16[8,512,128]{2,1,0:T(8,128)(2,1)S(1)}, bf16[8,512,128]{2,1,0:T(8,128)(2,1)}, u32[]{:S(2)}) copy-start(bf16[8,512,128]{2,1,0:T(8,128)(2,1)} %param.10) | copy-start | bytes 3145732
  6.5 6.5 %copy-start.3 = (s32[512,8]{0,1:T(8,128)S(1)}, s32[512,8]{0,1:T(8,128)}, u32[]{:S(2)}) copy-start(s32[512,8]{0,1:T(8,128)} %param.9) | copy-start | bytes 49156
  6.5 220.8 %all-gather.7.cloned.1.call-start = ((), (), s32[]{:S(2)}) async-start(), calls=%async_computation.2 | async-start | bytes 35651584 | tf_op jit(solution)/shard_map/all_gather | solution.py:17
  53.3 164.5 %collective-permute-start = (bf16[512,8,128]{2,0,1:T(8,128)(2,1)}, bf16[512,8,128]{2,0,1:T(8,128)(2,1)}, u32[]{:S(2)}, u32[]{:S(2)}) collective-permute-start(bf16[512,8,128]{2,0,1:T(8,128)(2,1)} %bitcast.4), channel_id=1, source_target_pairs={{0,2},{2,4},{4,6},{6,8},{8,10},{10,12},{12,14},{14,16},{16,18},{18... | collective-permute-start | bytes 3145736 | tf_op jit(solution)/shard_map/ppermute | solution.py:12
  56.6 236.2 %collective-permute-start.2 = (bf16[512,8,128]{0,2,1:T(8,128)(2,1)}, bf16[512,8,128]{0,2,1:T(8,128)(2,1)}, u32[]{:S(2)}, u32[]{:S(2)}) collective-permute-start(bf16[512,8,128]{0,2,1:T(8,128)(2,1)} %copy.57), channel_id=1, source_target_pairs={{0,2},{2,4},{4,6},{6,8},{8,10},{10,12},{12,14},{14,16},{16,18},{18... | collective-permute-start | bytes 3145736 | tf_op jit(solution)/shard_map/ppermute | solution.py:12
  61.2 234.9 %collective-permute-start.3 = (f32[8,512,128]{2,1,0:T(8,128)}, f32[8,512,128]{2,1,0:T(8,128)}, u32[]{:S(2)}, u32[]{:S(2)}) collective-permute-start(f32[8,512,128]{2,1,0:T(8,128)} %fusion.3), channel_id=1, source_target_pairs={{0,2},{2,4},{4,6},{6,8},{8,10},{10,12},{12,14},{14,16},{16,18},{18... | collective-permute-start | bytes 6291464 | tf_op jit(solution)/shard_map/ppermute | solution.py:12
  64.9 211.0 %collective-permute-start.1 = (f32[8,512]{1,0:T(8,128)S(1)}, f32[8,512]{1,0:T(8,128)S(1)}, u32[]{:S(2)}, u32[]{:S(2)}) collective-permute-start(f32[8,512]{1,0:T(8,128)S(1)} %convert_reduce_fusion), channel_id=1, source_target_pairs={{0,2},{2,4},{4,6},{6,8},{8,10},{10,12},{12,14},{14,16},{16,18},{18... | collective-permute-start | bytes 49160 | tf_op jit(solution)/shard_map/ppermute | solution.py:12
  79.5 226.4 %all-to-all-start = ((bf16[1024,2,1024]{2,0,1:T(8,128)(2,1)}), bf16[1024,2,1024]{2,0,1:T(8,128)(2,1)}, u32[]{:S(2)}, u32[]{:S(2)}) async-start(bf16[1024,2,1024]{2,0,1:T(8,128)(2,1)} %copy.63), calls=%async_computation | async-start | bytes 8388608 | tf_op jit(solution)/shard_map/all_to_all | solution.py:98
  85.3 258.0 %all-gather.5.cloned.1.call-start = ((), (), s32[]{:S(2)}) async-start(), calls=%async_computation.1 | async-start | bytes 3145728 | tf_op jit(solution)/shard_map/all_gather | solution.py:100
  85.3 132.4 %copy-start.2 = (bf16[512,8,128]{2,1,0:T(8,128)(2,1)S(1)}, bf16[512,8,128]{2,1,0:T(8,128)(2,1)}, u32[]{:S(2)}) copy-start(bf16[512,8,128]{2,1,0:T(8,128)(2,1)} %param.7) | copy-start | bytes 3145732
  275.9 11.5 %slice-start.2 = ((s8[8388608]{0:T(1024)(128)(4,1)}), s8[4194304]{0:T(1024)(128)(4,1)S(1)}, s32[]{:S(2)}) async-start(s8[8388608]{0:T(1024)(128)(4,1)} %bitcast.76), calls=%async_computation.5 | async-start | bytes 8388608
  275.9 13.7 %slice-start = ((s8[8388608]{0:T(1024)(128)(4,1)}), s8[4194304]{0:T(1024)(128)(4,1)S(1)}, s32[]{:S(2)}) async-start(s8[8388608]{0:T(1024)(128)(4,1)} %bitcast.74), calls=%async_computation.3 | async-start | bytes 8388608
  279.4 7.9 %slice-start.3 = ((s8[8388608]{0:T(1024)(128)(4,1)}), s8[4194304]{0:T(1024)(128)(4,1)S(1)}, s32[]{:S(2)}) async-start(s8[8388608]{0:T(1024)(128)(4,1)} %bitcast.76), calls=%async_computation.6 | async-start | bytes 8388608
  279.4 10.1 %slice-start.1 = ((s8[8388608]{0:T(1024)(128)(4,1)}), s8[4194304]{0:T(1024)(128)(4,1)S(1)}, s32[]{:S(2)}) async-start(s8[8388608]{0:T(1024)(128)(4,1)} %bitcast.74), calls=%async_computation.4 | async-start | bytes 8388608
  305.9 43.6 %copy-start.1 = (bf16[8,512,128]{2,1,0:T(8,128)(2,1)S(1)}, bf16[8,512,128]{2,1,0:T(8,128)(2,1)}, u32[]{:S(2)}) copy-start(bf16[8,512,128]{2,1,0:T(8,128)(2,1)} %param.10) | copy-start | bytes 3145732
Sparse Core Ops, SparseCore 0:
  13.2 214.1 all-gather.6
  306.0 37.2 all-gather.4
